TPU v7x, 32 devices: a whole 2x2x4 slice. The times are simulated.
32 devices in a mesh: row: 8 (over y, x, core), col: 4 (over z).
Axes of the slice: x: 2, y: 2, z: 4, core: 2. Of those that a mesh axis runs over, the one named last changes fastest.
Arguments:
- columns: float32 [4096, 8192], P('col', 'row'), may hold values from -64 to 64
- block_order: int32 [64], P('col'), may hold values from 0 to 63, as said below
Outputs:
- rotated: float32 [4096, 8192], P('col', 'row')
Inputs may be any that keep to these rules, and one draw needn't show every extreme that they name: block_order is a permutation of 0 .. 63 in which slots c * 16 to (c + 1) * 16 - 1 name blocks c * 16 to (c + 1) * 16 - 1.
All inputs are finite; a program needn't handle non-finite values.
Results may differ from a plain program's by a relative error of at most 0.00055.
Values sent between devices are 32-bit elements; how exact they have to be, the bound alone decides.
No kernel may reach another device: no remote copies, remote signals or barrier semaphores. Data moves between devices by JAX's collectives and lax.ppermute only.
A program may use at most 64 MiB of HBM per device.

v0:
```python
import jax
import jax.numpy as jnp
from jax import lax
from jax.sharding import PartitionSpec as P

BLOCK = 64
STEPS = 4


def shifted(value, axis, steps):
    count = lax.axis_size(axis)
    leading, last = (max(0, -steps), min(count, count - steps))
    return lax.ppermute(value, axis, [(source, source + steps) for source in range(leading, last)])


def make_systems(cross_sum, col_norms):
    highest = lax.Precision.HIGHEST
    top_norms = col_norms[:, :BLOCK][:, :, None]
    bottom_norms = col_norms[:, BLOCK:][:, None, :]
    spread = bottom_norms - top_norms
    radius = jnp.sqrt(spread * spread + 4.0 * cross_sum * cross_sum)
    scale_term = (top_norms + bottom_norms) / BLOCK
    coupling = (
        2.0
        * cross_sum
        * spread
        / (
            spread * spread
            + 4.0 * cross_sum * cross_sum
            + jnp.abs(spread) * radius
            + scale_term * scale_term
        )
    )
    identity = jnp.eye(BLOCK, dtype=jnp.float32)
    left_system = identity + jnp.einsum("pij,pkj->pik", coupling, coupling, precision=highest)
    right_system = identity + jnp.einsum("pji,pjk->pik", coupling, coupling, precision=highest)
    identities = jnp.broadcast_to(identity, coupling.shape)
    upper_half = jnp.concatenate([identities, coupling], axis=2)
    lower_half = jnp.concatenate([-jnp.transpose(coupling, (0, 2, 1)), identities], axis=2)
    systems = jnp.concatenate([left_system, right_system], axis=0)
    targets = jnp.concatenate([upper_half, lower_half], axis=0)
    return (systems, targets)


def solve_systems(systems, targets):
    factors = jnp.linalg.cholesky(systems)

    def solve_one(factor, target):
        return jax.scipy.linalg.cho_solve((factor, True), target)

    return jax.vmap(solve_one)(factors, targets)


def finish_turn(targets, solved_all):
    highest = lax.Precision.HIGHEST
    pairs = targets.shape[0] // 2
    solved = jnp.concatenate([solved_all[:pairs], solved_all[pairs:]], axis=1)
    plus_skew = jnp.concatenate([targets[:pairs], targets[pairs:]], axis=1)
    return jnp.einsum("pij,pjk->pik", plus_skew, solved, precision=highest)


def cayley_turn(cross_sum, col_norms):
    systems, targets = make_systems(cross_sum, col_norms)
    total = systems.shape[0]
    groups = lax.axis_size("row")
    share = -(-total // groups)
    start = lax.axis_index("row") * share
    mine_systems = lax.dynamic_slice_in_dim(systems, start, share, 0)
    mine_targets = lax.dynamic_slice_in_dim(targets, start, share, 0)
    mine_solved = solve_systems(mine_systems, mine_targets)
    gathered = lax.all_gather(mine_solved, "row", axis=0, tiled=True)
    return finish_turn(targets, gathered)


def local(columns, block_order):
    highest = lax.Precision.HIGHEST
    width, length = columns.shape
    count = width // BLOCK
    position = lax.axis_index("col")
    last_index = lax.axis_size("col") - 1
    local_index = block_order - position * block_order.shape[0]
    blocks = jnp.take(columns.reshape(count, BLOCK, length), local_index, axis=0)
    blocks = blocks.reshape(count // 2, 2 * BLOCK, length)
    for sweep_step in range(STEPS):
        cross_part = jnp.einsum(
            "pim,pjm->pij", blocks[:, :BLOCK], blocks[:, BLOCK:], precision=highest
        )
        norm_part = jnp.sum(blocks * blocks, axis=2)
        cross_sum, col_norms = lax.psum((cross_part, norm_part), "row")
        turn_matrix = cayley_turn(cross_sum, col_norms)
        turned = jnp.einsum("pij,pim->pjm", turn_matrix, blocks, precision=highest)
        top_blocks = turned[:, :BLOCK]
        bottom_blocks = turned[:, BLOCK:]
        from_left = shifted(top_blocks[-1], "col", 1)
        from_right = shifted(bottom_blocks[0], "col", -1)
        first_top = jnp.where(position == 0, top_blocks[0], from_left)
        second_top = jnp.where(position == 0, bottom_blocks[0], top_blocks[0])
        new_tops = jnp.concatenate([first_top[None], second_top[None], top_blocks[1:-1]], axis=0)
        last_bottom = jnp.where(position == last_index, top_blocks[-1], from_right)
        new_bottoms = jnp.concatenate([bottom_blocks[1:], last_bottom[None]], axis=0)
        blocks = jnp.concatenate([new_tops, new_bottoms], axis=1)
    return blocks.reshape(width, length)


def solution(mesh):
    placed = (P("col", "row"), P("col"))
    return jax.shard_map(
        local, mesh=mesh, in_specs=placed, out_specs=P("col", "row"), check_vma=False
    )
```

profile of v0, /device:TPU:0, one launch (start us, length us, event | category | flops | bytes accessed | tf_op | source)
XLA Modules:
  0.0 517.0 jit_solution(15705440596389083100)
XLA Ops:
  7.5 5.0 gather_fusion
  12.5 2.5 bitcast_select_fusion
  15.0 1.9 copy-done
  17.0 2.9 fusion
  19.9 2.7 multiply_reduce_fusion.3
  22.7 15.1 %psum.57 = f32[8,128]{1,0:T(8,128)S(1)} all-reduce(f32[8,128]{1,0:T(8,128)S(1)} %reduce_sum.39), channel_id=1, replica_groups=mesh['row'=8,'col'=4] {'row'}, use_global_device_ids=true, to_apply=%region_2.3 | all-reduce | flops 1024 | bytes 8192 | tf_op jit(solution)/shard_map/psum | solution.py:89
  38.1 38.6 %all-reduce.5.cloned.1.call-done = f32[8,64,64]{1,2,0:T(8,128)} async-done(((f32[8,64,64]{1,2,0:T(8,128)}), f32[8,64,64]{1,2,0:T(8,128)}) %all-reduce.5.cloned.1.call-update) | async-done | bytes 131088 | tf_op jit(solution)/shard_map/psum | solution.py:89
  76.6 1.2 negate_bitcast_fusion.3
  79.3 11.7 %custom-call.14 = f32[2,64,64]{2,1,0:T(8,128)S(1)} custom-call(f32[2,64,64]{2,1,0:T(8,128)S(1)} %fusion.135), custom_call_target="Cholesky" | custom-call | tf_op jit(solution)/shard_map/jit(cholesky)/cholesky | solution.py:46
  91.2 9.8 %custom-call.15 = f32[2,1,64,64]{2,3,1,0:T(8,128)S(1)} custom-call(f32[2,1,64,64]{3,2,1,0:T(8,128)S(1)} %select_bitcast_fusion.7), custom_call_target="InvertDiagBlocksLowerTriangular" | custom-call | tf_op jit(solution)/shard_map/vmap(jit(_cho_solve))/triangular_solve | solution.py:49
  101.7 9.8 %all_gather.12 = f32[16,64,128]{2,1,0:T(8,128)S(1)} all-gather(f32[2,64,128]{2,1,0:T(8,128)S(1)} %fusion.132), channel_id=1, replica_groups=mesh['row'=8,'col'=4] {'row'}, dimensions={0}, use_global_device_ids=true | all-gather | bytes 589824 | tf_op jit(solution)/shard_map/all_gather | solution.py:71
  111.6 1.2 fusion.40
  112.8 4.1 fusion.167
  116.9 2.0 copy-done.2
  119.0 3.4 collective-permute-start
  122.4 1.3 collective-permute-start.1
  123.7 1.6 slice.214
  125.4 1.5 slice.213
  126.9 1.6 collective-permute-done
  128.5 4.1 collective-permute-done.1
  132.6 1.1 select_bitcast_fusion.3
  134.5 2.9 fusion.3
  137.4 12.1 %psum.59 = f32[8,128]{1,0:T(8,128)S(1)} all-reduce(f32[8,128]{1,0:T(8,128)S(1)} %multiply_reduce_fusion.2), channel_id=1, replica_groups=mesh['row'=8,'col'=4] {'row'}, use_global_device_ids=true, to_apply=%region_7.10 | all-reduce | flops 1024 | bytes 8192 | tf_op jit(solution)/shard_map/psum | solution.py:89
  149.8 52.5 %all-reduce.7.cloned.1.call-done = f32[8,64,64]{1,2,0:T(8,128)} async-done(((f32[8,64,64]{1,2,0:T(8,128)}), f32[8,64,64]{1,2,0:T(8,128)}) %all-reduce.7.cloned.1.call-update) | async-done | bytes 131088 | tf_op jit(solution)/shard_map/psum | solution.py:89
  202.3 1.2 negate_bitcast_fusion.2
  205.6 1.5 fusion.131
  207.1 12.5 %custom-call.16 = f32[2,64,64]{2,1,0:T(8,128)S(1)} custom-call(f32[2,64,64]{2,1,0:T(8,128)} %fusion.131), custom_call_target="Cholesky" | custom-call | tf_op jit(solution)/shard_map/jit(cholesky)/cholesky | solution.py:46
  220.4 10.6 %custom-call.17 = f32[2,1,64,64]{2,3,1,0:T(8,128)S(1)} custom-call(f32[2,1,64,64]{3,2,1,0:T(8,128)} %select_bitcast_fusion.6), custom_call_target="InvertDiagBlocksLowerTriangular" | custom-call | tf_op jit(solution)/shard_map/vmap(jit(_cho_solve))/triangular_solve | solution.py:49
  231.6 9.2 %all_gather.13 = f32[16,64,128]{2,1,0:T(8,128)S(1)} all-gather(f32[2,64,128]{2,1,0:T(8,128)S(1)} %fusion.128), channel_id=1, replica_groups=mesh['row'=8,'col'=4] {'row'}, dimensions={0}, use_global_device_ids=true | all-gather | bytes 589824 | tf_op jit(solution)/shard_map/all_gather | solution.py:71
  240.8 1.2 fusion.37
  242.1 3.8 fusion.32
  246.0 3.4 collective-permute-start.2
  249.4 1.5 collective-permute-start.3
  251.2 4.2 collective-permute-done.2
  255.4 4.1 collective-permute-done.3
  260.4 2.9 fusion.12
  263.3 12.0 %psum.61 = f32[8,128]{1,0:T(8,128)S(1)} all-reduce(f32[8,128]{1,0:T(8,128)S(1)} %multiply_reduce_fusion.1), channel_id=1, replica_groups=mesh['row'=8,'col'=4] {'row'}, use_global_device_ids=true, to_apply=%region_10.13 | all-reduce | flops 1024 | bytes 8192 | tf_op jit(solution)/shard_map/psum | solution.py:89
  275.5 52.7 %all-reduce.9.cloned.1.call-done = f32[8,64,64]{1,2,0:T(8,128)} async-done(((f32[8,64,64]{1,2,0:T(8,128)}), f32[8,64,64]{1,2,0:T(8,128)}) %all-reduce.9.cloned.1.call-update) | async-done | bytes 131088 | tf_op jit(solution)/shard_map/psum | solution.py:89
  328.2 1.2 negate_bitcast_fusion.1
  330.8 0.7 copy.160
  331.5 1.5 fusion.127
  333.0 12.5 %custom-call.18 = f32[2,64,64]{2,1,0:T(8,128)S(1)} custom-call(f32[2,64,64]{2,1,0:T(8,128)} %fusion.127), custom_call_target="Cholesky" | custom-call | tf_op jit(solution)/shard_map/jit(cholesky)/cholesky | solution.py:46
  346.4 10.6 %custom-call.19 = f32[2,1,64,64]{2,3,1,0:T(8,128)S(1)} custom-call(f32[2,1,64,64]{3,2,1,0:T(8,128)} %select_bitcast_fusion.5), custom_call_target="InvertDiagBlocksLowerTriangular" | custom-call | tf_op jit(solution)/shard_map/vmap(jit(_cho_solve))/triangular_solve | solution.py:49
  357.5 9.4 %all_gather.14 = f32[16,64,128]{2,1,0:T(8,128)S(1)} all-gather(f32[2,64,128]{2,1,0:T(8,128)S(1)} %fusion.124), channel_id=1, replica_groups=mesh['row'=8,'col'=4] {'row'}, dimensions={0}, use_global_device_ids=true | all-gather | bytes 589824 | tf_op jit(solution)/shard_map/all_gather | solution.py:71
  367.0 1.2 fusion.34
  368.2 3.8 fusion.31
  372.1 3.4 collective-permute-start.4
  375.5 1.3 collective-permute-start.5
  377.2 4.4 collective-permute-done.4
  381.6 4.1 collective-permute-done.5
  386.3 2.9 fusion.21
  389.2 12.3 %psum.63 = f32[8,128]{1,0:T(8,128)S(1)} all-reduce(f32[8,128]{1,0:T(8,128)S(1)} %multiply_reduce_fusion), channel_id=1, replica_groups=mesh['row'=8,'col'=4] {'row'}, use_global_device_ids=true, to_apply=%region_13.16 | all-reduce | flops 1024 | bytes 8192 | tf_op jit(solution)/shard_map/psum | solution.py:89
  401.6 52.8 %all-reduce.11.cloned.1.call-done = f32[8,64,64]{1,2,0:T(8,128)} async-done(((f32[8,64,64]{1,2,0:T(8,128)}), f32[8,64,64]{1,2,0:T(8,128)}) %all-reduce.11.cloned.1.call-update) | async-done | bytes 131088 | tf_op jit(solution)/shard_map/psum | solution.py:89
  454.4 1.2 negate_bitcast_fusion
  456.9 11.7 %custom-call.20 = f32[2,64,64]{2,1,0:T(8,128)S(1)} custom-call(f32[2,64,64]{2,1,0:T(8,128)S(1)} %fusion.123), custom_call_target="Cholesky" | custom-call | tf_op jit(solution)/shard_map/jit(cholesky)/cholesky | solution.py:46
  468.9 9.8 %custom-call.21 = f32[2,1,64,64]{2,3,1,0:T(8,128)S(1)} custom-call(f32[2,1,64,64]{3,2,1,0:T(8,128)S(1)} %select_bitcast_fusion.4), custom_call_target="InvertDiagBlocksLowerTriangular" | custom-call | tf_op jit(solution)/shard_map/vmap(jit(_cho_solve))/triangular_solve | solution.py:49
  479.5 9.2 %all_gather.15 = f32[16,64,128]{2,1,0:T(8,128)S(1)} all-gather(f32[2,64,128]{2,1,0:T(8,128)S(1)} %fusion.120), channel_id=1, replica_groups=mesh['row'=8,'col'=4] {'row'}, dimensions={0}, use_global_device_ids=true | all-gather | bytes 589824 | tf_op jit(solution)/shard_map/all_gather | solution.py:71
  488.7 1.2 fusion.57
  489.9 3.8 fusion.30
  493.8 3.4 collective-permute-start.6
  497.2 1.3 collective-permute-start.7
  498.7 4.5 collective-permute-done.6
  503.3 4.1 collective-permute-done.7
  507.4 2.5 maximum_maximum_fusion.3
  (125 shorter events, 15.8 us)
Async XLA Ops:
  6.5 70.1 %all-reduce.5.cloned.1.call-start = ((), (), s32[]{:S(2)}) async-start(), calls=%async_computation | async-start | bytes 524288 | tf_op jit(solution)/shard_map/psum | solution.py:89
  15.0 1.9 copy-start
  19.8 182.5 %all-reduce.7.cloned.1.call-start = ((), (), s32[]{:S(2)}) async-start(), calls=%async_computation.1 | async-start | bytes 524288 | tf_op jit(solution)/shard_map/psum | solution.py:89
  101.1 11.7 %copy-start.1 = (f32[8,128,1024]{2,1,0:T(8,128)S(1)}, f32[8,128,1024]{2,1,0:T(8,128)}, u32[]{:S(2)}) copy-start(f32[8,128,1024]{2,1,0:T(8,128)} %copy-done) | copy-start | bytes 12582916
  116.9 2.0 copy-start.2
  119.0 15.2 %copy-start.9 = (f32[1,64,1024]{2,1,0:T(8,128)}, f32[1,64,1024]{2,1,0:T(8,128)S(1)}, u32[]{:S(2)}) copy-start(f32[1,64,1024]{2,1,0:T(8,128)S(1)} %get-tuple-element.35) | copy-start | bytes 786436
  119.0 9.5 %collective-permute-start = (f32[64,1024]{1,0:T(8,128)S(1)}, f32[64,1024]{1,0:T(8,128)S(1)}, u32[]{:S(2)}, u32[]{:S(2)}) collective-permute-start(f32[64,1024]{1,0:T(8,128)S(1)} %get-tuple-element.36), channel_id=1, source_target_pairs={{0,1},{1,2},{2,3},{4,5},{5,6},{6,7},{8,9},{9,10},{10,11},{12,13},{... | collective-permute-start | bytes 786440 | tf_op jit(solution)/shard_map/ppermute | solution.py:13
  122.4 10.2 %collective-permute-start.1 = (f32[64,1024]{1,0:T(8,128)S(1)}, f32[64,1024]{1,0:T(8,128)S(1)}, u32[]{:S(2)}, u32[]{:S(2)}) collective-permute-start(f32[64,1024]{1,0:T(8,128)S(1)} %get-tuple-element.34), channel_id=1, source_target_pairs={{1,0},{2,1},{3,2},{5,4},{6,5},{7,6},{9,8},{10,9},{11,10},{13,12},{... | collective-permute-start | bytes 786440 | tf_op jit(solution)/shard_map/ppermute | solution.py:13
  126.9 7.3 %copy-start.7 = (f32[6,64,1024]{2,1,0:T(8,128)}, f32[6,64,1024]{2,1,0:T(8,128)S(1)}, u32[]{:S(2)}) copy-start(f32[6,64,1024]{2,1,0:T(8,128)S(1)} %slice.213) | copy-start | bytes 4718596
  133.7 0.7 copy-start.17
  133.7 0.8 copy-start.19
  149.5 178.7 %all-reduce.9.cloned.1.call-start = ((), (), s32[]{:S(2)}) async-start(), calls=%async_computation.2 | async-start | bytes 524288 | tf_op jit(solution)/shard_map/psum | solution.py:89
  204.9 37.2 %copy-start.10 = (f32[1,64,1024]{2,1,0:T(8,128)S(1)}, f32[1,64,1024]{2,1,0:T(8,128)}, u32[]{:S(2)}) copy-start(f32[1,64,1024]{2,1,0:T(8,128)} %copy-done.9) | copy-start | bytes 786436
  204.9 37.1 %copy-start.18 = (f32[1,64,1024]{2,1,0:T(8,128)S(1)}, f32[1,64,1024]{2,1,0:T(8,128)}, u32[]{:S(2)}) copy-start(f32[1,64,1024]{2,1,0:T(8,128)} %copy-done.17) | copy-start | bytes 786436
  204.9 37.1 %copy-start.20 = (f32[1,64,1024]{2,1,0:T(8,128)S(1)}, f32[1,64,1024]{2,1,0:T(8,128)}, u32[]{:S(2)}) copy-start(f32[1,64,1024]{2,1,0:T(8,128)} %copy-done.19) | copy-start | bytes 786436
  231.0 11.0 %copy-start.8 = (f32[6,64,1024]{2,1,0:T(8,128)S(1)}, f32[6,64,1024]{2,1,0:T(8,128)}, u32[]{:S(2)}) copy-start(f32[6,64,1024]{2,1,0:T(8,128)} %copy-done.7) | copy-start | bytes 4718596
  246.0 14.2 %copy-start.11 = (f32[1,64,1024]{2,1,0:T(8,128)}, f32[1,64,1024]{2,1,0:T(8,128)S(1)}, u32[]{:S(2)}) copy-start(f32[1,64,1024]{2,1,0:T(8,128)S(1)} %get-tuple-element.30) | copy-start | bytes 786436
  246.0 9.5 %collective-permute-start.2 = (f32[64,1024]{1,0:T(8,128)S(1)}, f32[64,1024]{1,0:T(8,128)S(1)}, u32[]{:S(2)}, u32[]{:S(2)}) collective-permute-start(f32[64,1024]{1,0:T(8,128)S(1)} %get-tuple-element.31), channel_id=1, source_target_pairs={{0,1},{1,2},{2,3},{4,5},{5,6},{6,7},{8,9},{9,10},{10,11},{12,13},{... | collective-permute-start | bytes 786440 | tf_op jit(solution)/shard_map/ppermute | solution.py:13
  249.4 10.2 %collective-permute-start.3 = (f32[64,1024]{1,0:T(8,128)S(1)}, f32[64,1024]{1,0:T(8,128)S(1)}, u32[]{:S(2)}, u32[]{:S(2)}) collective-permute-start(f32[64,1024]{1,0:T(8,128)S(1)} %get-tuple-element.29), channel_id=1, source_target_pairs={{1,0},{2,1},{3,2},{5,4},{6,5},{7,6},{9,8},{10,9},{11,10},{13,12},{... | collective-permute-start | bytes 786440 | tf_op jit(solution)/shard_map/ppermute | solution.py:13
  251.2 8.9 %copy-start.5 = (f32[6,64,1024]{2,1,0:T(8,128)}, f32[6,64,1024]{2,1,0:T(8,128)S(1)}, u32[]{:S(2)}) copy-start(f32[6,64,1024]{2,1,0:T(8,128)S(1)} %slice.220) | copy-start | bytes 4718596
  259.6 0.7 copy-start.13
  259.6 0.8 copy-start.15
  275.4 179.0 %all-reduce.11.cloned.1.call-start = ((), (), s32[]{:S(2)}) async-start(), calls=%async_computation.3 | async-start | bytes 524288 | tf_op jit(solution)/shard_map/psum | solution.py:89
  330.8 37.4 %copy-start.12 = (f32[1,64,1024]{2,1,0:T(8,128)S(1)}, f32[1,64,1024]{2,1,0:T(8,128)}, u32[]{:S(2)}) copy-start(f32[1,64,1024]{2,1,0:T(8,128)} %copy-done.11) | copy-start | bytes 786436
  330.8 37.4 %copy-start.14 = (f32[1,64,1024]{2,1,0:T(8,128)S(1)}, f32[1,64,1024]{2,1,0:T(8,128)}, u32[]{:S(2)}) copy-start(f32[1,64,1024]{2,1,0:T(8,128)} %copy-done.13) | copy-start | bytes 786436
  330.8 37.4 %copy-start.16 = (f32[1,64,1024]{2,1,0:T(8,128)S(1)}, f32[1,64,1024]{2,1,0:T(8,128)}, u32[]{:S(2)}) copy-start(f32[1,64,1024]{2,1,0:T(8,128)} %copy-done.15) | copy-start | bytes 786436
  356.9 11.3 %copy-start.6 = (f32[6,64,1024]{2,1,0:T(8,128)S(1)}, f32[6,64,1024]{2,1,0:T(8,128)}, u32[]{:S(2)}) copy-start(f32[6,64,1024]{2,1,0:T(8,128)} %copy-done.5) | copy-start | bytes 4718596
  372.1 9.5 %collective-permute-start.4 = (f32[64,1024]{1,0:T(8,128)S(1)}, f32[64,1024]{1,0:T(8,128)S(1)}, u32[]{:S(2)}, u32[]{:S(2)}) collective-permute-start(f32[64,1024]{1,0:T(8,128)S(1)} %get-tuple-element.26), channel_id=1, source_target_pairs={{0,1},{1,2},{2,3},{4,5},{5,6},{6,7},{8,9},{9,10},{10,11},{12,13},{... | collective-permute-start | bytes 786440 | tf_op jit(solution)/shard_map/ppermute | solution.py:13
  375.5 10.2 %collective-permute-start.5 = (f32[64,1024]{1,0:T(8,128)S(1)}, f32[64,1024]{1,0:T(8,128)S(1)}, u32[]{:S(2)}, u32[]{:S(2)}) collective-permute-start(f32[64,1024]{1,0:T(8,128)S(1)} %get-tuple-element.24), channel_id=1, source_target_pairs={{1,0},{2,1},{3,2},{5,4},{6,5},{7,6},{9,8},{10,9},{11,10},{13,12},{... | collective-permute-start | bytes 786440 | tf_op jit(solution)/shard_map/ppermute | solution.py:13
  377.2 9.1 %copy-start.3 = (f32[6,64,1024]{2,1,0:T(8,128)}, f32[6,64,1024]{2,1,0:T(8,128)S(1)}, u32[]{:S(2)}) copy-start(f32[6,64,1024]{2,1,0:T(8,128)S(1)} %slice.227) | copy-start | bytes 4718596
  478.8 11.1 %copy-start.4 = (f32[6,64,1024]{2,1,0:T(8,128)S(1)}, f32[6,64,1024]{2,1,0:T(8,128)}, u32[]{:S(2)}) copy-start(f32[6,64,1024]{2,1,0:T(8,128)} %copy-done.3) | copy-start | bytes 4718596
  493.8 9.5 %collective-permute-start.6 = (f32[64,1024]{1,0:T(8,128)S(1)}, f32[64,1024]{1,0:T(8,128)S(1)}, u32[]{:S(2)}, u32[]{:S(2)}) collective-permute-start(f32[64,1024]{1,0:T(8,128)S(1)} %get-tuple-element.19), channel_id=1, source_target_pairs={{0,1},{1,2},{2,3},{4,5},{5,6},{6,7},{8,9},{9,10},{10,11},{12,13},{... | collective-permute-start | bytes 786440 | tf_op jit(solution)/shard_map/ppermute | solution.py:13
  497.2 10.2 %collective-permute-start.7 = (f32[64,1024]{1,0:T(8,128)S(1)}, f32[64,1024]{1,0:T(8,128)S(1)}, u32[]{:S(2)}, u32[]{:S(2)}) collective-permute-start(f32[64,1024]{1,0:T(8,128)S(1)} %get-tuple-element.20), channel_id=1, source_target_pairs={{1,0},{2,1},{3,2},{5,4},{6,5},{7,6},{9,8},{10,9},{11,10},{13,12},{... | collective-permute-start | bytes 786440 | tf_op jit(solution)/shard_map/ppermute | solution.py:13
Sparse Core Ops, SparseCore 0:
  20.0 56.6 all-reduce.4
  149.6 52.6 all-reduce.6
  275.5 52.6 all-reduce.8
  401.6 52.6 all-reduce.10
where the time goes:
time: 524 us; the launch traced here: 517 us
  waiting for transfers between devices  228 us (44%)
  other arithmetic  111 us (21%)
  blocking collectives  89.2 us (17%)
  matrix products  38.7 us (7%)
  starting transfers between devices  19.3 us (4%)
  local copies, waits for them, and re-layouts  16.6 us (3%)
  between operations  14.5 us (3%)
    psum x4, waiting for transfers between devices, local(): cross_sum, col_norms = lax.psum((cross_part, norm_part), 'row')  197 us
    psum x4, blocking collectives, local(): cross_sum, col_norms = lax.psum((cross_part, norm_part), 'row')  51.6 us
    another operation x13, other arithmetic, solve_systems(): factors = jnp.linalg.cholesky(systems)  49 us
    another operation x9, other arithmetic, solve_one(): return jax.scipy.linalg.cho_solve((factor, True), target)  42.4 us
    all_gather x4, blocking collectives, cayley_turn(): gathered = lax.all_gather(mine_solved, 'row', axis=0, tiled=True)  37.7 us
    ppermute x8, waiting for transfers between devices, shifted(): lax.ppermute(value, axis, [(source, source + steps) for source in range(l...  31.2 us
    ppermute x8, starting transfers between devices, shifted(): lax.ppermute(value, axis, [(source, source + steps) for source in range(l...  19 us
    dot_general x4, matrix products, local(): turned = jnp.einsum('pij,pim->pjm', turn_matrix, blocks, precision=highest)  15.6 us
  transfers between devices with their start and end apart: 12, of which 12 were waited for; matrix products, arithmetic and copies ran while one was open for 1% of the time, Pallas kernels for 0%

commit v1 on v0

--- a/solution.py
+++ b/solution.py
@@ -68,7 +68,12 @@
     mine_systems = lax.dynamic_slice_in_dim(systems, start, share, 0)
     mine_targets = lax.dynamic_slice_in_dim(targets, start, share, 0)
     mine_solved = solve_systems(mine_systems, mine_targets)
-    gathered = lax.all_gather(mine_solved, "row", axis=0, tiled=True)
+    ring = [mine_solved]
+    for hop in range(7):
+        ring.append(lax.ppermute(ring[-1], "row", [(dev, (dev + 1) % 8) for dev in range(8)]))
+    gathered = jnp.roll(
+        jnp.concatenate(ring[::-1], axis=0), (lax.axis_index("row") + 1) * ring[0].shape[0], axis=0
+    )
     return finish_turn(targets, gathered)
 
 

time: 524 us -> 606 us (1.16)
  waiting for transfers between devices: 228 us -> 347 us
  blocking collectives: 89.2 us -> 50.5 us
    ppermute x0 -> x28, waiting for transfers between devices: none -> 128 us  [cayley_turn(): lax.ppermute(ring[-1], 'row', [(dev, (dev + 1) % 8) for dev in range(8)])]
    all_gather x4 -> x0, blocking collectives: 37.7 us -> none  [cayley_turn(): gathered = lax.all_gather(mine_solved, 'row', axis=0, tiled=True)]
    ppermute x8, waiting for transfers between devices: 31.2 us -> 23.5 us  [shifted(): lax.ppermute(value, axis, [(source, source + steps) for source in range(l...]
  transfers between devices with their start and end apart: 12 -> 40, of which waited for: 12 -> 39; matrix products, arithmetic and copies ran while one was open for 1% -> 1% of each run, Pallas kernels for 0% -> 0%
where the time goes in v1:
time: 606 us; the launch traced here: 599 us
  waiting for transfers between devices  347 us (57%)
  other arithmetic  111 us (18%)
  blocking collectives  50.5 us (8%)
  matrix products  38.7 us (6%)
  starting transfers between devices  20.3 us (3%)
  local copies, waits for them, and re-layouts  16.9 us (3%)
  between operations  14.6 us (2%)
    psum x4, waiting for transfers between devices, local(): cross_sum, col_norms = lax.psum((cross_part, norm_part), 'row')  195 us
    ppermute x28, waiting for transfers between devices, cayley_turn(): lax.ppermute(ring[-1], 'row', [(dev, (dev + 1) % 8) for dev in range(8)])  128 us
    psum x4, blocking collectives, local(): cross_sum, col_norms = lax.psum((cross_part, norm_part), 'row')  50.5 us
    another operation x13, other arithmetic, solve_systems(): factors = jnp.linalg.cholesky(systems)  49 us
    another operation x9, other arithmetic, solve_one(): return jax.scipy.linalg.cho_solve((factor, True), target)  42.4 us
    ppermute x8, waiting for transfers between devices, shifted(): lax.ppermute(value, axis, [(source, source + steps) for source in range(l...  23.5 us
    ppermute x8, starting transfers between devices, shifted(): lax.ppermute(value, axis, [(source, source + steps) for source in range(l...  19 us
    dot_general x4, matrix products, local(): turned = jnp.einsum('pij,pim->pjm', turn_matrix, blocks, precision=highest)  15.6 us
  transfers between devices with their start and end apart: 40, of which 39 were waited for; matrix products, arithmetic and copies ran while one was open for 1% of the time, Pallas kernels for 0%

profile of v1, /device:TPU:0, one launch (start us, length us, event | category | flops | bytes accessed | tf_op | source)
XLA Modules:
  0.0 599.3 jit_solution(12522642322759520676)
XLA Ops:
  7.5 5.0 gather_fusion
  12.5 2.5 bitcast_select_fusion
  17.0 2.9 fusion
  19.9 2.7 multiply_reduce_fusion.3
  22.8 15.2 %psum.57 = f32[8,128]{1,0:T(8,128)S(1)} all-reduce(f32[8,128]{1,0:T(8,128)S(1)} %reduce_sum.39), channel_id=1, replica_groups=mesh['row'=8,'col'=4] {'row'}, use_global_device_ids=true, to_apply=%region_2.3 | all-reduce | flops 1024 | bytes 8192 | tf_op jit(solution)/shard_map/psum | solution.py:94
  38.1 38.6 %all-reduce.5.cloned.1.call-done = f32[8,64,64]{1,2,0:T(8,128)} async-done(((f32[8,64,64]{1,2,0:T(8,128)}), f32[8,64,64]{1,2,0:T(8,128)}) %all-reduce.5.cloned.1.call-update) | async-done | bytes 131088 | tf_op jit(solution)/shard_map/psum | solution.py:94
  79.3 11.7 %custom-call.14 = f32[2,64,64]{2,1,0:T(8,128)S(1)} custom-call(f32[2,64,64]{2,1,0:T(8,128)S(1)} %fusion.139), custom_call_target="Cholesky" | custom-call | tf_op jit(solution)/shard_map/jit(cholesky)/cholesky | solution.py:46
  91.3 9.8 %custom-call.15 = f32[2,1,64,64]{2,3,1,0:T(8,128)S(1)} custom-call(f32[2,1,64,64]{3,2,1,0:T(8,128)S(1)} %select_bitcast_fusion.7), custom_call_target="InvertDiagBlocksLowerTriangular" | custom-call | tf_op jit(solution)/shard_map/vmap(jit(_cho_solve))/triangular_solve | solution.py:49
  101.8 4.6 collective-permute-done
  106.4 4.6 collective-permute-done.1
  110.9 4.6 collective-permute-done.2
  115.5 4.6 collective-permute-done.3
  120.1 4.6 collective-permute-done.4
  124.7 4.6 collective-permute-done.5
  129.5 4.5 collective-permute-done.6
  135.5 4.1 fusion.171
  141.8 3.4 collective-permute-start.7
  149.7 3.8 collective-permute-done.8
  155.4 2.9 fusion.3
  158.3 11.8 %psum.59 = f32[8,128]{1,0:T(8,128)S(1)} all-reduce(f32[8,128]{1,0:T(8,128)S(1)} %multiply_reduce_fusion.2), channel_id=1, replica_groups=mesh['row'=8,'col'=4] {'row'}, use_global_device_ids=true, to_apply=%region_7.11 | all-reduce | flops 1024 | bytes 8192 | tf_op jit(solution)/shard_map/psum | solution.py:94
  170.2 52.4 %all-reduce.7.cloned.1.call-done = f32[8,64,64]{1,2,0:T(8,128)} async-done(((f32[8,64,64]{1,2,0:T(8,128)}), f32[8,64,64]{1,2,0:T(8,128)}) %all-reduce.7.cloned.1.call-update) | async-done | bytes 131088 | tf_op jit(solution)/shard_map/psum | solution.py:94
  227.3 12.5 %custom-call.16 = f32[2,64,64]{2,1,0:T(8,128)S(1)} custom-call(f32[2,64,64]{2,1,0:T(8,128)} %fusion.135), custom_call_target="Cholesky" | custom-call | tf_op jit(solution)/shard_map/jit(cholesky)/cholesky | solution.py:46
  240.6 10.6 %custom-call.17 = f32[2,1,64,64]{2,3,1,0:T(8,128)S(1)} custom-call(f32[2,1,64,64]{3,2,1,0:T(8,128)} %select_bitcast_fusion.6), custom_call_target="InvertDiagBlocksLowerTriangular" | custom-call | tf_op jit(solution)/shard_map/vmap(jit(_cho_solve))/triangular_solve | solution.py:49
  252.1 4.6 collective-permute-done.9
  256.6 4.6 collective-permute-done.10
  261.2 4.6 collective-permute-done.11
  265.8 4.6 collective-permute-done.12
  270.4 4.6 collective-permute-done.13
  275.0 4.6 collective-permute-done.14
  279.6 4.6 collective-permute-done.15
  285.7 3.8 fusion.32
  289.6 3.4 collective-permute-start.16
  296.9 4.4 collective-permute-done.17
  302.2 2.9 fusion.12
  305.1 11.8 %psum.61 = f32[8,128]{1,0:T(8,128)S(1)} all-reduce(f32[8,128]{1,0:T(8,128)S(1)} %multiply_reduce_fusion.1), channel_id=1, replica_groups=mesh['row'=8,'col'=4] {'row'}, use_global_device_ids=true, to_apply=%region_10.14 | all-reduce | flops 1024 | bytes 8192 | tf_op jit(solution)/shard_map/psum | solution.py:94
  317.4 51.9 %all-reduce.9.cloned.1.call-done = f32[8,64,64]{1,2,0:T(8,128)} async-done(((f32[8,64,64]{1,2,0:T(8,128)}), f32[8,64,64]{1,2,0:T(8,128)}) %all-reduce.9.cloned.1.call-update) | async-done | bytes 131088 | tf_op jit(solution)/shard_map/psum | solution.py:94
  374.1 12.5 %custom-call.18 = f32[2,64,64]{2,1,0:T(8,128)S(1)} custom-call(f32[2,64,64]{2,1,0:T(8,128)} %fusion.131), custom_call_target="Cholesky" | custom-call | tf_op jit(solution)/shard_map/jit(cholesky)/cholesky | solution.py:46
  387.4 10.6 %custom-call.19 = f32[2,1,64,64]{2,3,1,0:T(8,128)S(1)} custom-call(f32[2,1,64,64]{3,2,1,0:T(8,128)} %select_bitcast_fusion.5), custom_call_target="InvertDiagBlocksLowerTriangular" | custom-call | tf_op jit(solution)/shard_map/vmap(jit(_cho_solve))/triangular_solve | solution.py:49
  398.6 4.6 collective-permute-done.18
  403.2 4.6 collective-permute-done.19
  407.8 4.6 collective-permute-done.20
  412.4 4.6 collective-permute-done.21
  417.0 4.6 collective-permute-done.22
  421.6 4.6 collective-permute-done.23
  426.2 4.6 collective-permute-done.24
  432.3 3.8 fusion.31
  436.2 3.4 collective-permute-start.25
  443.4 4.4 collective-permute-done.26
  448.4 2.9 fusion.21
  451.3 11.8 %psum.63 = f32[8,128]{1,0:T(8,128)S(1)} all-reduce(f32[8,128]{1,0:T(8,128)S(1)} %multiply_reduce_fusion), channel_id=1, replica_groups=mesh['row'=8,'col'=4] {'row'}, use_global_device_ids=true, to_apply=%region_13.17 | all-reduce | flops 1024 | bytes 8192 | tf_op jit(solution)/shard_map/psum | solution.py:94
  463.2 52.4 %all-reduce.11.cloned.1.call-done = f32[8,64,64]{1,2,0:T(8,128)} async-done(((f32[8,64,64]{1,2,0:T(8,128)}), f32[8,64,64]{1,2,0:T(8,128)}) %all-reduce.11.cloned.1.call-update) | async-done | bytes 131088 | tf_op jit(solution)/shard_map/psum | solution.py:94
  518.1 11.7 %custom-call.20 = f32[2,64,64]{2,1,0:T(8,128)S(1)} custom-call(f32[2,64,64]{2,1,0:T(8,128)S(1)} %fusion.127), custom_call_target="Cholesky" | custom-call | tf_op jit(solution)/shard_map/jit(cholesky)/cholesky | solution.py:46
  530.1 9.8 %custom-call.21 = f32[2,1,64,64]{2,3,1,0:T(8,128)S(1)} custom-call(f32[2,1,64,64]{3,2,1,0:T(8,128)S(1)} %select_bitcast_fusion.4), custom_call_target="InvertDiagBlocksLowerTriangular" | custom-call | tf_op jit(solution)/shard_map/vmap(jit(_cho_solve))/triangular_solve | solution.py:49
  540.8 4.6 collective-permute-done.27
  545.4 4.6 collective-permute-done.28
  550.0 4.6 collective-permute-done.29
  554.5 4.6 collective-permute-done.30
  559.1 4.6 collective-permute-done.31
  563.7 4.6 collective-permute-done.32
  568.5 4.6 collective-permute-done.33
  574.6 3.8 fusion.30
  578.5 3.4 collective-permute-start.34
  585.7 4.4 collective-permute-done.35
  590.2 2.3 maximum_maximum_fusion.3
  (213 shorter events, 51.0 us)
Async XLA Ops:
  6.5 70.1 %all-reduce.5.cloned.1.call-start = ((), (), s32[]{:S(2)}) async-start(), calls=%async_computation | async-start | bytes 524288 | tf_op jit(solution)/shard_map/psum | solution.py:94
  15.0 2.0 copy-start
  19.9 202.7 %all-reduce.7.cloned.1.call-start = ((), (), s32[]{:S(2)}) async-start(), calls=%async_computation.1 | async-start | bytes 524288 | tf_op jit(solution)/shard_map/psum | solution.py:94
  101.7 4.6 collective-permute-start
  106.4 4.6 collective-permute-start.1
  110.9 4.6 collective-permute-start.2
  115.5 4.6 collective-permute-start.3
  120.1 4.6 collective-permute-start.4
  124.7 4.6 collective-permute-start.5
  129.3 4.7 collective-permute-start.6
  129.5 6.1 %copy-start.1 = (f32[8,128,1024]{2,1,0:T(8,128)S(1)}, f32[8,128,1024]{2,1,0:T(8,128)}, u32[]{:S(2)}) copy-start(f32[8,128,1024]{2,1,0:T(8,128)} %copy-done) | copy-start | bytes 12582916
  139.7 2.0 copy-start.2
  141.8 13.3 %copy-start.9 = (f32[1,64,1024]{2,1,0:T(8,128)}, f32[1,64,1024]{2,1,0:T(8,128)S(1)}, u32[]{:S(2)}) copy-start(f32[1,64,1024]{2,1,0:T(8,128)S(1)} %get-tuple-element.36) | copy-start | bytes 786436
  141.8 7.9 %collective-permute-start.7 = (f32[64,1024]{1,0:T(8,128)S(1)}, f32[64,1024]{1,0:T(8,128)S(1)}, u32[]{:S(2)}, u32[]{:S(2)}) collective-permute-start(f32[64,1024]{1,0:T(8,128)S(1)} %get-tuple-element.37), channel_id=1, source_target_pairs={{0,1},{1,2},{2,3},{4,5},{5,6},{6,7},{8,9},{9,10},{10,11},{12,13},{... | collective-permute-start | bytes 786440 | tf_op jit(solution)/shard_map/ppermute | solution.py:13
  145.2 8.3 %collective-permute-start.8 = (f32[64,1024]{1,0:T(8,128)S(1)}, f32[64,1024]{1,0:T(8,128)S(1)}, u32[]{:S(2)}, u32[]{:S(2)}) collective-permute-start(f32[64,1024]{1,0:T(8,128)S(1)} %get-tuple-element.35), channel_id=1, source_target_pairs={{1,0},{2,1},{3,2},{5,4},{6,5},{7,6},{9,8},{10,9},{11,10},{13,12},{... | collective-permute-start | bytes 786440 | tf_op jit(solution)/shard_map/ppermute | solution.py:13
  149.7 5.4 copy-start.7
  154.6 0.7 copy-start.17
  154.6 0.8 copy-start.19
  170.1 199.3 %all-reduce.9.cloned.1.call-start = ((), (), s32[]{:S(2)}) async-start(), calls=%async_computation.2 | async-start | bytes 524288 | tf_op jit(solution)/shard_map/psum | solution.py:94
  225.0 60.6 %copy-start.10 = (f32[1,64,1024]{2,1,0:T(8,128)S(1)}, f32[1,64,1024]{2,1,0:T(8,128)}, u32[]{:S(2)}) copy-start(f32[1,64,1024]{2,1,0:T(8,128)} %copy-done.9) | copy-start | bytes 786436
  225.1 60.6 %copy-start.18 = (f32[1,64,1024]{2,1,0:T(8,128)S(1)}, f32[1,64,1024]{2,1,0:T(8,128)}, u32[]{:S(2)}) copy-start(f32[1,64,1024]{2,1,0:T(8,128)} %copy-done.17) | copy-start | bytes 786436
  225.1 60.6 %copy-start.20 = (f32[1,64,1024]{2,1,0:T(8,128)S(1)}, f32[1,64,1024]{2,1,0:T(8,128)}, u32[]{:S(2)}) copy-start(f32[1,64,1024]{2,1,0:T(8,128)} %copy-done.19) | copy-start | bytes 786436
  251.2 34.5 %copy-start.8 = (f32[6,64,1024]{2,1,0:T(8,128)S(1)}, f32[6,64,1024]{2,1,0:T(8,128)}, u32[]{:S(2)}) copy-start(f32[6,64,1024]{2,1,0:T(8,128)} %copy-done.7) | copy-start | bytes 4718596
  251.8 4.9 collective-permute-start.9
  256.6 4.6 collective-permute-start.10
  261.2 4.6 collective-permute-start.11
  265.8 4.6 collective-permute-start.12
  270.4 4.6 collective-permute-start.13
  275.0 4.6 collective-permute-start.14
  279.6 4.6 collective-permute-start.15
  289.6 12.3 %copy-start.11 = (f32[1,64,1024]{2,1,0:T(8,128)}, f32[1,64,1024]{2,1,0:T(8,128)S(1)}, u32[]{:S(2)}) copy-start(f32[1,64,1024]{2,1,0:T(8,128)S(1)} %get-tuple-element.31) | copy-start | bytes 786436
  289.6 7.3 %collective-permute-start.16 = (f32[64,1024]{1,0:T(8,128)S(1)}, f32[64,1024]{1,0:T(8,128)S(1)}, u32[]{:S(2)}, u32[]{:S(2)}) collective-permute-start(f32[64,1024]{1,0:T(8,128)S(1)} %get-tuple-element.32), channel_id=1, source_target_pairs={{0,1},{1,2},{2,3},{4,5},{5,6},{6,7},{8,9},{9,10},{10,11},{12,13},{... | collective-permute-start | bytes 786440 | tf_op jit(solution)/shard_map/ppermute | solution.py:13
  293.0 8.3 %collective-permute-start.17 = (f32[64,1024]{1,0:T(8,128)S(1)}, f32[64,1024]{1,0:T(8,128)S(1)}, u32[]{:S(2)}, u32[]{:S(2)}) collective-permute-start(f32[64,1024]{1,0:T(8,128)S(1)} %get-tuple-element.30), channel_id=1, source_target_pairs={{1,0},{2,1},{3,2},{5,4},{6,5},{7,6},{9,8},{10,9},{11,10},{13,12},{... | collective-permute-start | bytes 786440 | tf_op jit(solution)/shard_map/ppermute | solution.py:13
  294.6 7.2 %copy-start.5 = (f32[6,64,1024]{2,1,0:T(8,128)}, f32[6,64,1024]{2,1,0:T(8,128)S(1)}, u32[]{:S(2)}) copy-start(f32[6,64,1024]{2,1,0:T(8,128)S(1)} %slice.220) | copy-start | bytes 4718596
  301.4 0.7 copy-start.13
  301.4 0.8 copy-start.15
  316.9 198.7 %all-reduce.11.cloned.1.call-start = ((), (), s32[]{:S(2)}) async-start(), calls=%async_computation.3 | async-start | bytes 524288 | tf_op jit(solution)/shard_map/psum | solution.py:94
  371.9 60.4 %copy-start.12 = (f32[1,64,1024]{2,1,0:T(8,128)S(1)}, f32[1,64,1024]{2,1,0:T(8,128)}, u32[]{:S(2)}) copy-start(f32[1,64,1024]{2,1,0:T(8,128)} %copy-done.11) | copy-start | bytes 786436
  371.9 60.3 %copy-start.14 = (f32[1,64,1024]{2,1,0:T(8,128)S(1)}, f32[1,64,1024]{2,1,0:T(8,128)}, u32[]{:S(2)}) copy-start(f32[1,64,1024]{2,1,0:T(8,128)} %copy-done.13) | copy-start | bytes 786436
  371.9 60.3 %copy-start.16 = (f32[1,64,1024]{2,1,0:T(8,128)S(1)}, f32[1,64,1024]{2,1,0:T(8,128)}, u32[]{:S(2)}) copy-start(f32[1,64,1024]{2,1,0:T(8,128)} %copy-done.15) | copy-start | bytes 786436
  398.0 34.3 %copy-start.6 = (f32[6,64,1024]{2,1,0:T(8,128)S(1)}, f32[6,64,1024]{2,1,0:T(8,128)}, u32[]{:S(2)}) copy-start(f32[6,64,1024]{2,1,0:T(8,128)} %copy-done.5) | copy-start | bytes 4718596
  398.6 4.6 collective-permute-start.18
  403.2 4.6 collective-permute-start.19
  407.8 4.6 collective-permute-start.20
  412.4 4.6 collective-permute-start.21
  417.0 4.6 collective-permute-start.22
  421.6 4.6 collective-permute-start.23
  426.2 4.6 collective-permute-start.24
  436.2 7.3 %collective-permute-start.25 = (f32[64,1024]{1,0:T(8,128)S(1)}, f32[64,1024]{1,0:T(8,128)S(1)}, u32[]{:S(2)}, u32[]{:S(2)}) collective-permute-start(f32[64,1024]{1,0:T(8,128)S(1)} %get-tuple-element.27), channel_id=1, source_target_pairs={{0,1},{1,2},{2,3},{4,5},{5,6},{6,7},{8,9},{9,10},{10,11},{12,13},{... | collective-permute-start | bytes 786440 | tf_op jit(solution)/shard_map/ppermute | solution.py:13
  439.6 8.3 %collective-permute-start.26 = (f32[64,1024]{1,0:T(8,128)S(1)}, f32[64,1024]{1,0:T(8,128)S(1)}, u32[]{:S(2)}, u32[]{:S(2)}) collective-permute-start(f32[64,1024]{1,0:T(8,128)S(1)} %get-tuple-element.25), channel_id=1, source_target_pairs={{1,0},{2,1},{3,2},{5,4},{6,5},{7,6},{9,8},{10,9},{11,10},{13,12},{... | collective-permute-start | bytes 786440 | tf_op jit(solution)/shard_map/ppermute | solution.py:13
  441.4 7.0 %copy-start.3 = (f32[6,64,1024]{2,1,0:T(8,128)}, f32[6,64,1024]{2,1,0:T(8,128)S(1)}, u32[]{:S(2)}) copy-start(f32[6,64,1024]{2,1,0:T(8,128)S(1)} %slice.227) | copy-start | bytes 4718596
  540.1 34.5 %copy-start.4 = (f32[6,64,1024]{2,1,0:T(8,128)S(1)}, f32[6,64,1024]{2,1,0:T(8,128)}, u32[]{:S(2)}) copy-start(f32[6,64,1024]{2,1,0:T(8,128)} %copy-done.3) | copy-start | bytes 4718596
  540.7 4.6 collective-permute-start.27
  545.4 4.6 collective-permute-start.28
  550.0 4.6 collective-permute-start.29
  554.5 4.6 collective-permute-start.30
  559.1 4.6 collective-permute-start.31
  563.7 4.6 collective-permute-start.32
  568.3 4.8 collective-permute-start.33
  578.5 7.3 %collective-permute-start.34 = (f32[64,1024]{1,0:T(8,128)S(1)}, f32[64,1024]{1,0:T(8,128)S(1)}, u32[]{:S(2)}, u32[]{:S(2)}) collective-permute-start(f32[64,1024]{1,0:T(8,128)S(1)} %get-tuple-element.20), channel_id=1, source_target_pairs={{0,1},{1,2},{2,3},{4,5},{5,6},{6,7},{8,9},{9,10},{10,11},{12,13},{... | collective-permute-start | bytes 786440 | tf_op jit(solution)/shard_map/ppermute | solution.py:13
  581.9 8.3 %collective-permute-start.35 = (f32[64,1024]{1,0:T(8,128)S(1)}, f32[64,1024]{1,0:T(8,128)S(1)}, u32[]{:S(2)}, u32[]{:S(2)}) collective-permute-start(f32[64,1024]{1,0:T(8,128)S(1)} %get-tuple-element.21), channel_id=1, source_target_pairs={{1,0},{2,1},{3,2},{5,4},{6,5},{7,6},{9,8},{10,9},{11,10},{13,12},{... | collective-permute-start | bytes 786440 | tf_op jit(solution)/shard_map/ppermute | solution.py:13
Sparse Core Ops, SparseCore 0:
  20.0 56.6 all-reduce.4
  170.2 52.3 all-reduce.6
  317.0 52.3 all-reduce.8
  463.2 52.3 all-reduce.10
